TPU v7x, 32 devices: a whole 2x2x4 slice. The times are simulated.
32 devices in a mesh: grp: 8 (over y, x, core), shard: 4 (over z).
Axes of the slice: x: 2, y: 2, z: 4, core: 2. Of those that a mesh axis runs over, the one named last changes fastest.
Arguments:
- gradients: bfloat16 [8, 1024, 5120], P('grp', None, 'shard'), may hold values from -150 to 150
- left_factor: bfloat16 [8, 1024, 1024], P('grp'), may hold values from -1 to 2, as said below
- right_factor: bfloat16 [8, 5120, 5120], P('grp', 'shard'), may hold values from -1 to 2, as said below
Outputs:
- update: bfloat16 [8, 1024, 5120], P('grp', None, 'shard')
Inputs may be any that keep to these rules, and one draw needn't show every extreme that they name: `left_factor`: each factor is upper triangular with a positive diagonal. `right_factor`: each factor is upper triangular with a positive diagonal.
All inputs are finite; a program needn't handle non-finite values.
Results may differ from a plain program's by a relative error of at most 0.0061.
Values may be sent and summed in bfloat16 or wider, within the bound.
A program may use at most 128 MiB of HBM per device.

v0:
```python
import jax
import jax.numpy as jnp
from jax import lax
from jax.sharding import PartitionSpec as P


def body(gradients, left_factor, right_factor):
    squares = jnp.float32(0.0)
    gradient = gradients[0]
    left_q = left_factor[0]
    right_rows = right_factor[0]
    block = right_rows
    first = lax.dot_general(
        lax.all_gather(gradient, "shard", axis=1, tiled=True),
        block,
        (((1,), (1,)), ((), ())),
        preferred_element_type=jnp.float32,
    ).astype(jnp.bfloat16)
    block = right_rows
    second_rows = lax.psum_scatter(
        lax.dot_general(block, first, (((0,), (1,)), ((), ())), preferred_element_type=jnp.float32),
        "shard",
        scatter_dimension=0,
        tiled=True,
    ).astype(jnp.bfloat16)
    second = second_rows.T
    third = jnp.dot(left_q, second, preferred_element_type=jnp.float32).astype(jnp.bfloat16)
    precond = lax.dot_general(
        left_q, third, (((0,), (0,)), ((), ())), preferred_element_type=jnp.float32
    )
    results = [precond]
    squares = jnp.sum(precond * precond)
    total = lax.psum(squares, ("grp", "shard"))
    count = (
        gradients.shape[0]
        * lax.axis_size("grp")
        * gradients.shape[1]
        * gradients.shape[2]
        * lax.axis_size("shard")
    )
    rms = jnp.sqrt(total / count + 1e-06)
    factor = jnp.minimum(jnp.float32(1.0), 1.1 / rms)
    stacked = jnp.stack(results, axis=0)
    return (stacked * factor).astype(jnp.bfloat16)


def solution(mesh):
    in_specs = (P("grp", None, "shard"), P("grp", None, None), P("grp", "shard", None))
    out_specs = P("grp", None, "shard")
    return jax.shard_map(body, mesh=mesh, in_specs=in_specs, out_specs=out_specs, check_vma=False)
```

profile of v0, /device:TPU:0, one launch (start us, length us, event | category | flops | bytes accessed | tf_op | source)
XLA Modules:
  0.0 647.6 jit_solution(3090217392802980609)
XLA Ops:
  6.5 0.0 copy-start
  6.5 0.0 all-gather.3.cloned.1.call-start
  6.5 0.7 all-gather.3.cloned.1.call-update
  7.3 0.0 reduce-scatter.2.cloned.1.call-start
  7.3 188.3 %all-gather.3.cloned.1.call-done = bf16[1,1024,5120]{2,1,0:T(8,128)(2,1)} async-done(((bf16[1,1024,1280]{2,1,0:T(8,128)(2,1)}), bf16[1,1024,5120]{2,1,0:T(8,128)(2,1)}) %all-gather.3.cloned.1.call-update) | async-done | bytes 10485776 | tf_op jit(solution)/shard_map/all_gather | solution.py:14
  195.6 17.5 %fusion.8 = bf16[1024,1280]{1,0:T(8,128)(2,1)S(1)} fusion(bf16[1,1280,5120]{2,1,0:T(8,128)(2,1)} %param.5, bf16[1,1024,5120]{2,1,0:T(8,128)(2,1)} %all-gather.3.cloned.1.call-done), kind=kOutput, calls=%fused_computation.8 | convolution fusion | flops 13423083520 | bytes 26214400 | tf_op jit(solution)/shard_map/dot_general | solution.py:13
  213.0 20.6 %fusion.4 = f32[5120,1024]{0,1:T(8,128)} fusion(bf16[1024,1280]{1,0:T(8,128)(2,1)S(1)} %fusion.8, bf16[1,1280,5120]{2,1,0:T(8,128)(2,1)} %param.5), kind=kOutput, calls=%fused_computation.4 | convolution fusion | flops 13421772800 | bytes 36700160 | tf_op jit(solution)/shard_map/dot_general | solution.py:21
  233.6 0.0 reduce-scatter.2.cloned.1.call-update
  233.7 345.7 %reduce-scatter.2.cloned.1.call-done = f32[1280,1024]{0,1:T(8,128)} async-done(((f32[5120,1024]{0,1:T(8,128)}), f32[1280,1024]{0,1:T(8,128)}) %reduce-scatter.2.cloned.1.call-update) | async-done | bytes 5242896 | tf_op jit(solution)/shard_map/reduce_scatter | solution.py:20
  579.4 0.0 copy-done
  579.4 9.9 %multiply_reduce_fusion = (f32[]{:T(128)}, f32[1280,1024]{1,0:T(8,128)}) fusion(bf16[1,1024,1024]{2,1,0:T(8,128)(2,1)S(1)} %copy-done, f32[1280,1024]{0,1:T(8,128)} %reduce-scatter.2.cloned.1.call-done), kind=kOutput, calls=%fused_computation.7 | convolution fusion | flops 5373952000 | bytes 12582916 | tf_op jit(solution)/shard_map/dot_general | solution.py:28
  589.3 41.7 %psum.7 = f32[]{:T(128)} all-reduce(f32[]{:T(128)} %get-tuple-element.5), channel_id=1, replica_groups=mesh['grp'=8,'shard'=4] {'grp','shard'}, use_global_device_ids=true, to_apply=%region_2.0 | all-reduce | flops 1 | bytes 8 | tf_op jit(solution)/shard_map/psum | solution.py:33
  631.7 4.7 fusion.13
  636.4 4.4 copy.4
Async XLA Ops:
  6.5 572.8 %copy-start = (bf16[1,1024,1024]{2,1,0:T(8,128)(2,1)S(1)}, bf16[1,1024,1024]{2,1,0:T(8,128)(2,1)}, u32[]{:S(2)}) copy-start(bf16[1,1024,1024]{2,1,0:T(8,128)(2,1)} %param.4) | copy-start | bytes 6291460
  6.5 189.0 %all-gather.3.cloned.1.call-start = ((), (), s32[]{:S(2)}) async-start(), calls=%async_computation.2 | async-start | bytes 13107200 | tf_op jit(solution)/shard_map/all_gather | solution.py:14
  7.3 572.1 %reduce-scatter.2.cloned.1.call-start = ((), (), s32[]{:S(2)}) async-start(), calls=%async_computation.1 | async-start | bytes 26214400 | tf_op jit(solution)/shard_map/reduce_scatter | solution.py:20
Sparse Core Ops, SparseCore 0:
  8.9 186.6 all-gather.2
  233.8 345.5 reduce-scatter.1
where the time goes:
time: 648 us
  waiting for transfers between devices  535 us (83%)
  matrix products  48 us (7%)
  blocking collectives  41.7 us (6%)
  between operations  14.1 us (2%)
    reduce_scatter x1, waiting for transfers between devices, body(): lax.psum_scatter(lax.dot_general(block, first, (((0,), (1,)), ((), ())),...  346 us
    all_gather x1, waiting for transfers between devices, body(): lax.all_gather(gradient, 'shard', axis=1, tiled=True)  188 us
    psum x1, blocking collectives, body(): total = lax.psum(squares, ('grp', 'shard'))  41.7 us
    dot_general x1, matrix products, body(): lax.dot_general(block, first, (((0,), (1,)), ((), ())), preferred_element...  20.6 us
    dot_general x1, matrix products, body(): lax.dot_general(lax.all_gather(gradient, 'shard', axis=1, tiled=True), bl...  17.5 us
  transfers between devices with their start and end apart: 2, of which 2 were waited for; matrix products, arithmetic and copies ran while one was open for 0% of the time, Pallas kernels for 0%

commit v1 on v0

--- a/solution.py
+++ b/solution.py
@@ -30,7 +30,7 @@
     )
     results = [precond]
     squares = jnp.sum(precond * precond)
-    total = lax.psum(squares, ("grp", "shard"))
+    total = lax.psum(lax.psum(squares, "shard"), "grp")
     count = (
         gradients.shape[0]
         * lax.axis_size("grp")

time: 648 us -> 631 us (0.974)
  blocking collectives: 41.7 us -> 24.8 us
    psum x1 -> x2, blocking collectives: 41.7 us -> 24.8 us  [body(): total = lax.psum(lax.psum(squares, 'shard'), 'grp')]
where the time goes in v1:
time: 631 us
  waiting for transfers between devices  535 us (85%)
  matrix products  48 us (8%)
  blocking collectives  24.8 us (4%)
  between operations  14.1 us (2%)
    reduce_scatter x1, waiting for transfers between devices, body(): lax.psum_scatter(lax.dot_general(block, first, (((0,), (1,)), ((), ())),...  346 us
    all_gather x1, waiting for transfers between devices, body(): lax.all_gather(gradient, 'shard', axis=1, tiled=True)  188 us
    psum x2, blocking collectives, body(): total = lax.psum(lax.psum(squares, 'shard'), 'grp')  24.8 us
    dot_general x1, matrix products, body(): lax.dot_general(block, first, (((0,), (1,)), ((), ())), preferred_element...  20.6 us
    dot_general x1, matrix products, body(): lax.dot_general(lax.all_gather(gradient, 'shard', axis=1, tiled=True), bl...  17.5 us
  transfers between devices with their start and end apart: 2, of which 2 were waited for; matrix products, arithmetic and copies ran while one was open for 0% of the time, Pallas kernels for 0%

profile of v1, /device:TPU:0, one launch (start us, length us, event | category | flops | bytes accessed | tf_op | source)
XLA Modules:
  0.0 630.7 jit_solution(1604368660793829187)
XLA Ops:
  6.5 0.0 copy-start
  6.5 0.0 all-gather.3.cloned.1.call-start
  6.5 0.7 all-gather.3.cloned.1.call-update
  7.3 0.0 reduce-scatter.2.cloned.1.call-start
  7.3 188.3 %all-gather.3.cloned.1.call-done = bf16[1,1024,5120]{2,1,0:T(8,128)(2,1)} async-done(((bf16[1,1024,1280]{2,1,0:T(8,128)(2,1)}), bf16[1,1024,5120]{2,1,0:T(8,128)(2,1)}) %all-gather.3.cloned.1.call-update) | async-done | bytes 10485776 | tf_op jit(solution)/shard_map/all_gather | solution.py:14
  195.6 17.5 %fusion.8 = bf16[1024,1280]{1,0:T(8,128)(2,1)S(1)} fusion(bf16[1,1280,5120]{2,1,0:T(8,128)(2,1)} %param.5, bf16[1,1024,5120]{2,1,0:T(8,128)(2,1)} %all-gather.3.cloned.1.call-done), kind=kOutput, calls=%fused_computation.8 | convolution fusion | flops 13423083520 | bytes 26214400 | tf_op jit(solution)/shard_map/dot_general | solution.py:13
  213.0 20.6 %fusion.4 = f32[5120,1024]{0,1:T(8,128)} fusion(bf16[1024,1280]{1,0:T(8,128)(2,1)S(1)} %fusion.8, bf16[1,1280,5120]{2,1,0:T(8,128)(2,1)} %param.5), kind=kOutput, calls=%fused_computation.4 | convolution fusion | flops 13421772800 | bytes 36700160 | tf_op jit(solution)/shard_map/dot_general | solution.py:21
  233.6 0.0 reduce-scatter.2.cloned.1.call-update
  233.7 345.7 %reduce-scatter.2.cloned.1.call-done = f32[1280,1024]{0,1:T(8,128)} async-done(((f32[5120,1024]{0,1:T(8,128)}), f32[1280,1024]{0,1:T(8,128)}) %reduce-scatter.2.cloned.1.call-update) | async-done | bytes 5242896 | tf_op jit(solution)/shard_map/reduce_scatter | solution.py:20
  579.4 0.0 copy-done
  579.4 9.9 %multiply_reduce_fusion = (f32[]{:T(128)}, f32[1280,1024]{1,0:T(8,128)}) fusion(bf16[1,1024,1024]{2,1,0:T(8,128)(2,1)S(1)} %copy-done, f32[1280,1024]{0,1:T(8,128)} %reduce-scatter.2.cloned.1.call-done), kind=kOutput, calls=%fused_computation.7 | convolution fusion | flops 5373952000 | bytes 12582916 | tf_op jit(solution)/shard_map/dot_general | solution.py:28
  589.3 12.4 %psum.14 = f32[]{:T(128)} all-reduce(f32[]{:T(128)} %get-tuple-element.5), channel_id=1, replica_groups=mesh['grp'=8,'shard'=4] {'shard'}, use_global_device_ids=true, to_apply=%region_2.0 | all-reduce | flops 1 | bytes 8 | tf_op jit(solution)/shard_map/psum | solution.py:33
  601.7 12.4 %psum.15 = f32[]{:T(128)} all-reduce(f32[]{:T(128)} %psum.14), channel_id=1, replica_groups=mesh['grp'=8,'shard'=4] {'grp'}, use_global_device_ids=true, to_apply=%region_3.0 | all-reduce | flops 1 | bytes 8 | tf_op jit(solution)/shard_map/psum | solution.py:33
  614.8 4.7 fusion.13
  619.5 4.4 copy.4
Async XLA Ops:
  6.5 572.8 %copy-start = (bf16[1,1024,1024]{2,1,0:T(8,128)(2,1)S(1)}, bf16[1,1024,1024]{2,1,0:T(8,128)(2,1)}, u32[]{:S(2)}) copy-start(bf16[1,1024,1024]{2,1,0:T(8,128)(2,1)} %param.4) | copy-start | bytes 6291460
  6.5 189.0 %all-gather.3.cloned.1.call-start = ((), (), s32[]{:S(2)}) async-start(), calls=%async_computation.2 | async-start | bytes 13107200 | tf_op jit(solution)/shard_map/all_gather | solution.py:14
  7.3 572.1 %reduce-scatter.2.cloned.1.call-start = ((), (), s32[]{:S(2)}) async-start(), calls=%async_computation.1 | async-start | bytes 26214400 | tf_op jit(solution)/shard_map/reduce_scatter | solution.py:20
Sparse Core Ops, SparseCore 0:
  8.9 186.6 all-gather.2
  233.8 345.5 reduce-scatter.1

commit v2 on v0

--- a/solution.py
+++ b/solution.py
@@ -11,7 +11,7 @@
     right_rows = right_factor[0]
     block = right_rows
     first = lax.dot_general(
-        lax.all_gather(gradient, "shard", axis=1, tiled=True),
+        jnp.concatenate(lax.all_gather(gradient, "shard"), axis=1),
         block,
         (((1,), (1,)), ((), ())),
         preferred_element_type=jnp.float32,

time: 648 us -> 663 us (1.023)
  local copies, waits for them, and re-layouts: 4.38 us -> 18.8 us
    all_gather x0 -> x1, local copies, waits for them, and re-layouts: none -> 14.4 us  [body(): lax.all_gather(gradient, 'shard')]
where the time goes in v2:
time: 663 us; the launch traced here: 662 us
  waiting for transfers between devices  535 us (81%)
  matrix products  48.1 us (7%)
  blocking collectives  41.7 us (6%)
  local copies, waits for them, and re-layouts  18.8 us (3%)
  between operations  14.1 us (2%)
    reduce_scatter x1, waiting for transfers between devices, body(): lax.psum_scatter(lax.dot_general(block, first, (((0,), (1,)), ((), ())),...  346 us
    all_gather x1, waiting for transfers between devices, body(): lax.all_gather(gradient, 'shard')  188 us
    psum x1, blocking collectives, body(): total = lax.psum(squares, ('grp', 'shard'))  41.7 us
    dot_general x1, matrix products, body(): lax.dot_general(block, first, (((0,), (1,)), ((), ())), preferred_element...  20.6 us
    dot_general x1, matrix products, body(): lax.dot_general(jnp.concatenate(lax.all_gather(gradient, 'shard'), axis=1...  17.6 us
    all_gather x1, local copies, waits for them, and re-layouts, body(): lax.all_gather(gradient, 'shard')  14.4 us
  transfers between devices with their start and end apart: 2, of which 2 were waited for; matrix products, arithmetic and copies ran while one was open for 0% of the time, Pallas kernels for 0%

profile of v2, /device:TPU:0, one launch (start us, length us, event | category | flops | bytes accessed | tf_op | source)
XLA Modules:
  0.0 662.1 jit_solution(1887197203822806031)
XLA Ops:
  6.5 0.0 copy-start
  6.5 0.0 all-gather.2.cloned.1.call-start
  6.5 0.7 all-gather.2.cloned.1.call-update
  7.3 0.0 reduce-scatter.2.cloned.1.call-start
  7.3 188.3 %all-gather.2.cloned.1.call-done = bf16[4,1024,1280]{2,1,0:T(8,128)(2,1)} async-done(((bf16[1,1024,1280]{2,1,0:T(8,128)(2,1)}), bf16[4,1024,1280]{2,1,0:T(8,128)(2,1)}) %all-gather.2.cloned.1.call-update) | async-done | bytes 10485776 | tf_op jit(solution)/shard_map/all_gather | solution.py:14
  195.6 14.4 %copy.7 = bf16[4,1024,1280]{1,2,0:T(8,128)(2,1)} copy(bf16[4,1024,1280]{2,1,0:T(8,128)(2,1)} %all-gather.2.cloned.1.call-done) | data formatting | bytes 20971520 | tf_op jit(solution)/shard_map/all_gather | solution.py:14
  209.9 17.6 %fusion.7 = bf16[1024,1280]{1,0:T(8,128)(2,1)S(1)} fusion(bf16[1024,5120]{0,1:T(8,128)(2,1)} %bitcast.31, bf16[1,1280,5120]{2,1,0:T(8,128)(2,1)} %param.5), kind=kOutput, calls=%fused_computation.7 | convolution fusion | flops 13423083520 | bytes 26214400 | tf_op jit(solution)/shard_map/dot_general | solution.py:13
  227.5 20.6 %fusion.4 = f32[5120,1024]{0,1:T(8,128)} fusion(bf16[1024,1280]{1,0:T(8,128)(2,1)S(1)} %fusion.7, bf16[1,1280,5120]{2,1,0:T(8,128)(2,1)} %param.5), kind=kOutput, calls=%fused_computation.4 | convolution fusion | flops 13421772800 | bytes 36700160 | tf_op jit(solution)/shard_map/dot_general | solution.py:21
  248.1 0.0 reduce-scatter.2.cloned.1.call-update
  248.1 345.7 %reduce-scatter.2.cloned.1.call-done = f32[1280,1024]{0,1:T(8,128)} async-done(((f32[5120,1024]{0,1:T(8,128)}), f32[1280,1024]{0,1:T(8,128)}) %reduce-scatter.2.cloned.1.call-update) | async-done | bytes 5242896 | tf_op jit(solution)/shard_map/reduce_scatter | solution.py:20
  593.8 0.0 copy-done
  593.8 9.9 %multiply_reduce_fusion = (f32[]{:T(128)}, f32[1280,1024]{1,0:T(8,128)}) fusion(bf16[1,1024,1024]{2,1,0:T(8,128)(2,1)S(1)} %copy-done, f32[1280,1024]{0,1:T(8,128)} %reduce-scatter.2.cloned.1.call-done), kind=kOutput, calls=%fused_computation.6 | convolution fusion | flops 5373952000 | bytes 12582916 | tf_op jit(solution)/shard_map/dot_general | solution.py:28
  603.8 41.7 %psum.7 = f32[]{:T(128)} all-reduce(f32[]{:T(128)} %get-tuple-element.5), channel_id=1, replica_groups=mesh['grp'=8,'shard'=4] {'grp','shard'}, use_global_device_ids=true, to_apply=%region_2.0 | all-reduce | flops 1 | bytes 8 | tf_op jit(solution)/shard_map/psum | solution.py:33
  646.1 4.7 fusion.10
  650.9 4.4 copy.8
Async XLA Ops:
  6.5 587.3 %copy-start = (bf16[1,1024,1024]{2,1,0:T(8,128)(2,1)S(1)}, bf16[1,1024,1024]{2,1,0:T(8,128)(2,1)}, u32[]{:S(2)}) copy-start(bf16[1,1024,1024]{2,1,0:T(8,128)(2,1)} %param.4) | copy-start | bytes 6291460
  6.5 189.0 %all-gather.2.cloned.1.call-start = ((), (), s32[]{:S(2)}) async-start(), calls=%async_computation.1 | async-start | bytes 13107200 | tf_op jit(solution)/shard_map/all_gather | solution.py:14
  7.3 586.6 %reduce-scatter.2.cloned.1.call-start = ((), (), s32[]{:S(2)}) async-start(), calls=%async_computation.2 | async-start | bytes 26214400 | tf_op jit(solution)/shard_map/reduce_scatter | solution.py:20
Sparse Core Ops, SparseCore 0:
  8.9 186.6 all-gather.1
  248.3 345.5 reduce-scatter.1
